TPU v7x, 32 devices: a whole 2x2x4 slice. The times are simulated.
32 devices in a mesh: band: 16 (over z, y, core), chan: 2 (over x).
Axes of the slice: x: 2, y: 2, z: 4, core: 2. Of those that a mesh axis runs over, the one named last changes fastest.
Arguments:
- fine_features: bfloat16 [2, 192, 128, 512], P(None, 'chan', 'band'), may hold values from -100 to 100
- coarse_level: bfloat16 [2, 256, 64, 256], P(None, 'chan', 'band'), may hold values from -100 to 100
- lat_weight: bfloat16 [256, 192], P('chan'), may hold values from -0.4375 to 0.4375
- lat_gain: bfloat16 [256], P('chan'), may hold values from 0.099609375 to 1.8984375
- lat_shift: bfloat16 [256], P('chan'), may hold values from -3 to 3
- out_weight: bfloat16 [3, 3, 256, 256], P(None, None, 'chan'), may hold values from -0.125 to 0.125
- out_gain: bfloat16 [256], P('chan'), may hold values from 0.099609375 to 1.8984375
- out_shift: bfloat16 [256], P('chan'), may hold values from -3 to 3
- mask_weight: bfloat16 [256, 256], P('chan'), may hold values from -0.375 to 0.375
- mask_bias: bfloat16 [256], P('chan'), may hold values from -1.796875 to 1.796875
- queries: bfloat16 [200, 256], replicated, may hold values from -128 to 128
Outputs:
- log_probs: float32 [2, 200, 128, 512], P(None, None, ('band', 'chan'))
All inputs are finite; a program needn't handle non-finite values.
Results may differ from a plain program's by a relative error of at most 0.0058.
Values may be sent and summed in bfloat16 or wider, within the bound.
A program may use at most 128 MiB of HBM per device.

v0:
```python
import jax
import jax.numpy as jnp
from jax import lax
from jax.sharding import PartitionSpec as P

D = 256
GROUPS = 32


epsilon = 1e-05


def extended_2(cells, sides, width):
    for axis, dim in sides:
        count = lax.axis_size(axis)
        ends = count - 1
        head = lax.slice_in_dim(cells, 0, width, axis=dim)
        tail = lax.slice_in_dim(cells, cells.shape[dim] - width, cells.shape[dim], axis=dim)
        cells = jnp.concatenate(
            [
                lax.ppermute(tail, axis, [(i, (i + 1) % count) for i in range(ends)]),
                cells,
                lax.ppermute(head, axis, [((i + 1) % count, i) for i in range(ends)]),
            ],
            axis=dim,
        )
    return cells


def interp(padded, axis):
    length = padded.shape[axis] - 2
    before = lax.slice_in_dim(padded, 0, length, axis=axis)
    middle = lax.slice_in_dim(padded, 1, length + 1, axis=axis)
    after = lax.slice_in_dim(padded, 2, length + 2, axis=axis)
    even_part = 0.25 * before + 0.75 * middle
    odd_part = 0.75 * middle + 0.25 * after
    paired = jnp.stack([even_part, odd_part], axis + 1)
    new_shape = list(middle.shape)
    new_shape[axis] = 2 * length
    return paired.reshape(new_shape)


def conv_taps(taps_weight, padded, row_count, col_count):
    summed = None
    for row_tap in range(3):
        for col_tap in range(3):
            window = padded[:, :, row_tap : row_tap + row_count, col_tap : col_tap + col_count]
            term = jnp.einsum(
                "oc,ncrw->norw",
                taps_weight[row_tap, col_tap],
                window,
                preferred_element_type=jnp.float32,
            )
            summed = term if summed is None else summed + term
    return summed


def apply_norm(blocks, mean_value, variance, full_shape, gain, shift):
    scaled = (
        (blocks - mean_value[:, :, None]) * lax.rsqrt(variance[:, :, None] + epsilon)
    ).reshape(full_shape)
    return (
        scaled * gain.astype(jnp.float32)[None, :, None, None]
        + shift.astype(jnp.float32)[None, :, None, None]
    )


def per_device(
    fine_features,
    coarse_level,
    lat_weight,
    lat_gain,
    lat_shift,
    out_weight,
    out_gain,
    out_shift,
    mask_weight,
    mask_bias,
    queries,
):
    images, in_share, band_rows, columns = fine_features.shape
    out_share = lat_weight.shape[0]
    group_size = D // GROUPS
    band_count = lax.axis_size("band")
    pixel_count = float(group_size * band_rows * band_count * columns)
    lateral = jnp.einsum(
        "oc,ncrw->norw",
        lat_weight,
        lax.all_gather(fine_features, "chan", axis=1, tiled=True),
        preferred_element_type=jnp.float32,
    )
    lat_blocks = lateral.reshape(images, out_share // group_size, -1)
    lat_mean = lax.psum(jnp.sum(lat_blocks, 2), "band") / pixel_count
    deviation = lat_blocks - lat_mean[:, :, None]
    lat_var = lax.psum(jnp.sum(deviation * deviation, 2), "band") / pixel_count
    lat_normed = apply_norm(lat_blocks, lat_mean, lat_var, lateral.shape, lat_gain, lat_shift)
    band_index = lax.axis_index("band")
    extended = extended_2(coarse_level, (("band", 2),), 1)
    top_row = jnp.where(band_index == 0, extended[:, :, 1:2], extended[:, :, 0:1])
    bottom_row = jnp.where(band_index == band_count - 1, extended[:, :, -2:-1], extended[:, :, -1:])
    extended = jnp.concatenate([top_row, extended[:, :, 1:-1], bottom_row], 2).astype(jnp.float32)
    extended = jnp.pad(extended, ((0, 0), (0, 0), (0, 0), (1, 1)), mode="edge")
    upsampled = interp(interp(extended, 2), 3)
    joined = (lat_normed + upsampled).astype(jnp.bfloat16)
    row_joined = lax.all_to_all(joined, "chan", split_axis=2, concat_axis=1, tiled=True)
    conv_weight, full_gain, full_shift, full_mask, full_bias = (
        lax.all_gather(out_weight, "chan", axis=2, tiled=True),
        lax.all_gather(out_gain, "chan", axis=0, tiled=True),
        lax.all_gather(out_shift, "chan", axis=0, tiled=True),
        lax.all_gather(mask_weight, "chan", axis=0, tiled=True),
        lax.all_gather(mask_bias, "chan", axis=0, tiled=True),
    )
    row_count = row_joined.shape[2]
    padded = extended_2(row_joined, ((("band", "chan"), 2),), 1)
    padded = jnp.pad(padded, ((0, 0), (0, 0), (0, 0), (1, 1)))
    conv_out = conv_taps(conv_weight, padded, row_count, columns)
    local_groups = conv_out.shape[1] // group_size
    conv_blocks = conv_out.reshape(images, local_groups, -1)
    out_mean = lax.psum(jnp.sum(conv_blocks, 2), ("band", "chan")) / pixel_count
    deviation = conv_blocks - out_mean[:, :, None]
    out_var = lax.psum(jnp.sum(deviation * deviation, 2), ("band", "chan")) / pixel_count
    activated = jnp.maximum(
        apply_norm(conv_blocks, out_mean, out_var, conv_out.shape, full_gain, full_shift), 0.0
    ).astype(jnp.bfloat16)
    mixed = jnp.einsum("oc,ncrw->norw", full_mask, activated, preferred_element_type=jnp.float32)
    features = (mixed + full_bias.astype(jnp.float32)[None, :, None, None]).astype(jnp.bfloat16)
    logits = jnp.einsum("qc,ncrw->nqrw", queries, features, preferred_element_type=jnp.float32)
    peak = jnp.max(logits, axis=1, keepdims=True)
    shifted = logits - peak
    return shifted - jnp.log(jnp.sum(jnp.exp(shifted), axis=1, keepdims=True))


def solution(mesh):
    return jax.shard_map(
        per_device,
        mesh=mesh,
        in_specs=(
            P(None, "chan", "band", None),
            P(None, "chan", "band", None),
            P("chan", None),
            P("chan"),
            P("chan"),
            P(None, None, "chan", None),
            P("chan"),
            P("chan"),
            P("chan", None),
            P("chan"),
            P(),
        ),
        out_specs=P(None, None, ("band", "chan"), None),
        check_vma=False,
    )
```

profile of v0, /device:TPU:0, one launch (start us, length us, event | category | flops | bytes accessed | tf_op | source)
XLA Modules:
  0.0 355.2 jit_solution(3142790244294858030)
XLA Ops:
  6.6 3.1 copy.21
  10.1 2.4 collective-permute-start
  12.6 1.3 collective-permute-start.1
  13.9 4.2 %collective-permute-done.1 = bf16[2,128,1,256]{3,2,1,0:T(2,128)(2,1)S(1)} collective-permute-done((bf16[2,128,1,256]{3,2,1,0:T(2,128)(2,1)S(1)}, bf16[2,128,1,256]{3,2,1,0:T(2,128)(2,1)S(1)}, u32[]{:S(2)}, u32[]{:S(2)}) %collective-permute-start.1) | collective-permute-done | bytes 131104 | tf_op jit(solution)/shard_map/ppermute | solution.py:23
  18.1 0.8 broadcast_select_fusion.1
  18.9 0.8 maximum_convert_fusion.6
  20.1 1.1 pad_maximum_fusion.1
  21.2 1.0 fusion.43
  22.2 2.4 pad_maximum_fusion.2
  24.6 3.2 copy.22
  28.8 5.2 %copy.23 = f32[2,128,8,256,2]{1,4,3,2,0:T(2,128)} copy(f32[2,128,8,256,2]{1,3,2,0,4:T(8,128)S(1)} %pad_maximum_fusion) | data formatting | bytes 8388608 | tf_op jit(solution)/shard_map/stack | solution.py:37
  34.0 23.6 %all-gather.6.cloned.1.call-done = bf16[2,192,8,512]{3,1,2,0:T(8,128)(2,1)} async-done(((bf16[2,96,8,512]{3,1,2,0:T(8,128)(2,1)}), bf16[2,192,8,512]{3,1,2,0:T(8,128)(2,1)}) %all-gather.6.cloned.1.call-update) | async-done | bytes 3145744 | tf_op jit(solution)/shard_map/all_gather | solution.py:89
  57.5 5.4 %bitcast_reduce_fusion.1 = (f32[2,128]{1,0:T(2,128)S(1)}, f32[2,8,512,128]{3,2,1,0:T(8,128)}) fusion(bf16[2,192,8,512]{3,1,2,0:T(8,128)(2,1)} %all-gather.6.cloned.1.call-done, bf16[128,192]{0,1:T(8,128)(2,1)S(1)} %copy-done.5), kind=kOutput, calls=%fused_computation.7 | convolution fusion | flops 403701504 | bytes 7390208 | tf_op jit(solution)/shard_map/oc,ncrw->norw/dot_general | solution.py:86
  63.1 33.2 %psum.28 = f32[2,16]{1,0:T(2,128)S(1)} all-reduce(f32[2,16]{1,0:T(2,128)S(1)} %reduce_sum.59), channel_id=1, replica_groups=mesh['band'=16,'chan'=2] {'band'}, use_global_device_ids=true, to_apply=%region_2.0 | all-reduce | flops 32 | bytes 256 | tf_op jit(solution)/shard_map/psum | solution.py:93
  96.5 2.8 multiply_reduce_fusion.1
  99.4 29.5 %psum.29 = f32[2,16]{1,0:T(2,128)S(1)} all-reduce(f32[2,16]{1,0:T(2,128)S(1)} %reduce_sum.62), channel_id=1, replica_groups=mesh['band'=16,'chan'=2] {'band'}, use_global_device_ids=true, to_apply=%region_5.6 | all-reduce | flops 32 | bytes 256 | tf_op jit(solution)/shard_map/psum | solution.py:95
  129.0 4.3 %add_convert_fusion.1 = bf16[2,128,8,512]{1,3,2,0:T(8,128)(2,1)S(1)} fusion(f32[2,128,8,512]{1,3,2,0:T(8,128)} %bitcast.138, f32[2,8,512,128]{3,2,1,0:T(8,128)} %get-tuple-element.18, f32[128]{0:T(128)S(1)} %convert_element_type.33, f32[128]{0:T(128)S(1)} %convert_element_type.32, f32[2,128]{1,0:T(2,128)S(1)} %mul.72, f32[2,128]{1,0:T(2,128)S(1)} %sub.53), kind=kLoop, calls=%fused_computation.12 | loop fusion | flops 6291456 | bytes 10488832 | tf_op jit(solution)/shard_map/convert_element_type | solution.py:104
  133.4 1.5 copy.24
  134.9 3.8 %all-to-all-start = ((bf16[2,128,8,512]{1,3,0,2:T(8,128)(2,1)}), bf16[2,128,8,512]{1,3,0,2:T(8,128)(2,1)S(1)}, u32[]{:S(2)}, u32[]{:S(2)}) async-start(bf16[2,128,8,512]{1,3,0,2:T(8,128)(2,1)} %copy.24), calls=%async_computation | async-start | bytes 4194304 | tf_op jit(solution)/shard_map/all_to_all | solution.py:105
  138.7 0.7 all-gather.8.cloned.1.call-update
  139.4 37.0 %all-to-all-done = bf16[2,128,8,512]{1,3,0,2:T(8,128)(2,1)S(1)} async-done(((bf16[2,128,8,512]{1,3,0,2:T(8,128)(2,1)}), bf16[2,128,8,512]{1,3,0,2:T(8,128)(2,1)S(1)}, u32[]{:S(2)}, u32[]{:S(2)}) %all-to-all-start) | async-done | bytes 2097184 | tf_op jit(solution)/shard_map/all_to_all | solution.py:105
  176.4 3.5 copy.42
  179.9 3.2 all_to_all.16
  183.1 1.1 fusion.58
  184.2 2.2 collective-permute-start.2
  186.4 11.5 %all-gather = bf16[2,1,128]{2,1,0:T(2,128)(2,1)S(1)} all-gather(bf16[1,1,128]{2,1,0:T(2,128)(2,1)S(1)} %bitcast.144), channel_id=1, replica_groups=mesh['band'=16,'chan'=2] {'chan'}, dimensions={0}, use_global_device_ids=true | all-gather | bytes 768 | tf_op jit(solution)/shard_map/all_gather | solution.py:108
  198.0 4.2 %all-gather.1 = bf16[2,1,128]{2,1,0:T(2,128)(2,1)S(1)} all-gather(bf16[1,1,128]{2,1,0:T(2,128)(2,1)S(1)} %bitcast.145), channel_id=1, replica_groups=mesh['band'=16,'chan'=2] {'chan'}, dimensions={0}, use_global_device_ids=true | all-gather | bytes 768 | tf_op jit(solution)/shard_map/all_gather | solution.py:109
  202.2 4.2 %all-gather.2 = bf16[2,1,128]{2,1,0:T(2,128)(2,1)S(1)} all-gather(bf16[1,1,128]{2,1,0:T(2,128)(2,1)S(1)} %bitcast.146), channel_id=1, replica_groups=mesh['band'=16,'chan'=2] {'chan'}, dimensions={0}, use_global_device_ids=true | all-gather | bytes 768 | tf_op jit(solution)/shard_map/all_gather | solution.py:111
  206.4 4.9 %all_gather.22 = bf16[256,256]{1,0:T(8,128)(2,1)S(1)} all-gather(bf16[128,256]{1,0:T(8,128)(2,1)S(1)} %copy-done.4), channel_id=1, replica_groups=mesh['band'=16,'chan'=2] {'chan'}, dimensions={0}, use_global_device_ids=true | all-gather | bytes 196608 | tf_op jit(solution)/shard_map/all_gather | solution.py:110
  211.4 1.3 collective-permute-start.3
  212.7 1.7 fusion.44
  214.5 2.7 fusion.7
  217.2 9.8 %collective-permute-done.3 = bf16[2,256,1,512]{1,3,2,0:T(8,128)(2,1)S(1)} collective-permute-done((bf16[2,256,1,512]{1,3,2,0:T(8,128)(2,1)}, bf16[2,256,1,512]{1,3,2,0:T(8,128)(2,1)S(1)}, u32[]{:S(2)}, u32[]{:S(2)}) %collective-permute-start.3) | collective-permute-done | bytes 524320 | tf_op jit(solution)/shard_map/ppermute | solution.py:23
  226.9 1.0 fusion.6
  227.9 2.7 fusion.11
  230.6 2.7 fusion.19
  233.3 2.7 fusion.21
  236.0 2.7 fusion.23
  238.7 2.7 fusion.25
  241.5 2.8 fusion.27
  244.2 0.7 copy-done.1
  244.9 11.3 %bitcast_reduce_fusion = (f32[2,256]{1,0:T(2,128)S(1)}, f32[2,4,512,256]{3,2,1,0:T(8,128)}) fusion(bf16[3,3,256,256]{3,2,1,0:T(8,128)(2,1)} %all-gather.8.cloned.1.call-done, bf16[2,256,6,514]{1,3,2,0:T(8,128)(2,1)S(1)} %fusion.6, f32[2,4,512,256]{3,2,1,0:T(8,128)} %fusion.11, f32[2,4,512,256]{3,2,1,0:T(8,128)} %fusion.19, f32[2,4,512,256]{3,2,1,0:T(8,128)} %fusion.21, ...), kind=kOutput, calls=%fused_computation.5 | convolution fusion | flops 546307584 | bytes 39979008 | tf_op jit(solution)/shard_map/oc,ncrw->norw/dot_general | solution.py:48
  256.4 37.0 %psum.30 = f32[2,32]{1,0:T(2,128)S(1)} all-reduce(f32[2,32]{1,0:T(2,128)S(1)} %reduce_sum.81), channel_id=1, replica_groups=mesh['band'=16,'chan'=2] {'band','chan'}, use_global_device_ids=true, to_apply=%region_8.9 | all-reduce | flops 64 | bytes 512 | tf_op jit(solution)/shard_map/psum | solution.py:119
  293.6 2.7 multiply_reduce_fusion
  296.4 40.9 %psum.31 = f32[2,32]{1,0:T(2,128)S(1)} all-reduce(f32[2,32]{1,0:T(2,128)S(1)} %reduce_sum.84), channel_id=1, replica_groups=mesh['band'=16,'chan'=2] {'band','chan'}, use_global_device_ids=true, to_apply=%region_11.12 | all-reduce | flops 64 | bytes 512 | tf_op jit(solution)/shard_map/psum | solution.py:121
  337.5 3.7 %fusion.33 = f32[2,4,512,200]{2,3,1,0:T(8,128)S(1)} fusion(f32[2,4,512,256]{3,2,1,0:T(8,128)} %get-tuple-element.20, f32[256]{0:T(256)S(1)} %bitcast.143, f32[256]{0:T(256)S(1)} %bitcast.142, f32[256]{0:T(256)S(1)} %bitcast.141, f32[2,256]{1,0:T(2,128)S(1)} %mul.85, f32[2,256]{1,0:T(2,128)S(1)} %sub.57, bf16[256,256]{1,0:T(8,128)(2,1)S(1)} %all_gather.22, ...), kind=kOutput, calls=%fused_computation.52 | convolution fusion | flops 964689920 | bytes 7711744 | tf_op jit(solution)/shard_map/qc,ncrw->nqrw/dot_general | solution.py:127
  341.2 2.9 exponential_reduce_fusion
  344.6 3.8 %copy.27 = f32[2,200,4,512]{3,2,1,0:T(4,128)} copy(f32[2,200,4,512]{3,1,2,0:T(8,128)S(1)} %log_subtract_fusion) | data formatting | bytes 6553600 | tf_op jit(solution)/shard_map/sub | solution.py:130
  (57 shorter events, 3.6 us)
Async XLA Ops:
  6.5 331.0 %copy-start = (bf16[200,256]{1,0:T(8,128)(2,1)S(1)}, bf16[200,256]{1,0:T(8,128)(2,1)}, u32[]{:S(2)}) copy-start(bf16[200,256]{1,0:T(8,128)(2,1)} %param.21) | copy-start | bytes 307204
  6.5 3.2 copy-start.2
  6.5 7.3 %copy-start.6 = (bf16[128]{0:T(256)(128)(2,1)S(1)}, bf16[128]{0:T(256)(128)(2,1)}, u32[]{:S(2)}) copy-start(bf16[128]{0:T(256)(128)(2,1)} %param.14) | copy-start | bytes 772
  6.5 7.3 %copy-start.7 = (bf16[128]{0:T(256)(128)(2,1)S(1)}, bf16[128]{0:T(256)(128)(2,1)}, u32[]{:S(2)}) copy-start(bf16[128]{0:T(256)(128)(2,1)} %param.15) | copy-start | bytes 772
  6.5 51.0 %all-gather.6.cloned.1.call-start = ((), (), s32[]{:S(2)}) async-start(), calls=%async_computation.1 | async-start | bytes 4718592 | tf_op jit(solution)/shard_map/all_gather | solution.py:89
  10.1 3.8 %collective-permute-start = (bf16[2,128,1,256]{3,2,1,0:T(2,128)(2,1)S(1)}, bf16[2,128,1,256]{3,2,1,0:T(2,128)(2,1)S(1)}, u32[]{:S(2)}, u32[]{:S(2)}) collective-permute-start(bf16[2,128,1,256]{3,2,1,0:T(2,128)(2,1)S(1)} %get-tuple-element.15), channel_id=1, source_target_pairs={{0,2},{2,4},{4,6},{6,8},{8,10},{10,12},{12,14},{14,16},{16,18},{18... | collective-permute-start | bytes 393224 | tf_op jit(solution)/shard_map/ppermute | solution.py:21
  12.6 5.5 %collective-permute-start.1 = (bf16[2,128,1,256]{3,2,1,0:T(2,128)(2,1)S(1)}, bf16[2,128,1,256]{3,2,1,0:T(2,128)(2,1)S(1)}, u32[]{:S(2)}, u32[]{:S(2)}) collective-permute-start(bf16[2,128,1,256]{3,2,1,0:T(2,128)(2,1)S(1)} %get-tuple-element.16), channel_id=1, source_target_pairs={{2,0},{4,2},{6,4},{8,6},{10,8},{12,10},{14,12},{16,14},{18,16},{20... | collective-permute-start | bytes 393224 | tf_op jit(solution)/shard_map/ppermute | solution.py:23
  28.8 28.8 %copy-start.5 = (bf16[128,192]{0,1:T(8,128)(2,1)S(1)}, bf16[128,192]{0,1:T(8,128)(2,1)}, u32[]{:S(2)}) copy-start(bf16[128,192]{0,1:T(8,128)(2,1)} %param.13) | copy-start | bytes 147460
  134.9 41.5 %all-to-all-start = ((bf16[2,128,8,512]{1,3,0,2:T(8,128)(2,1)}), bf16[2,128,8,512]{1,3,0,2:T(8,128)(2,1)S(1)}, u32[]{:S(2)}, u32[]{:S(2)}) async-start(bf16[2,128,8,512]{1,3,0,2:T(8,128)(2,1)} %copy.24), calls=%async_computation | async-start | bytes 4194304 | tf_op jit(solution)/shard_map/all_to_all | solution.py:105
  138.6 74.0 %all-gather.8.cloned.1.call-start = ((), (), s32[]{:S(2)}) async-start(), calls=%async_computation.2 | async-start | bytes 1769472 | tf_op jit(solution)/shard_map/all_gather | solution.py:107
  179.9 6.5 %copy-start.8 = (bf16[128]{0:T(256)(128)(2,1)S(1)}, bf16[128]{0:T(256)(128)(2,1)}, u32[]{:S(2)}) copy-start(bf16[128]{0:T(256)(128)(2,1)} %param.17) | copy-start | bytes 772
  179.9 18.1 %copy-start.9 = (bf16[128]{0:T(256)(128)(2,1)S(1)}, bf16[128]{0:T(256)(128)(2,1)}, u32[]{:S(2)}) copy-start(bf16[128]{0:T(256)(128)(2,1)} %param.18) | copy-start | bytes 772
  179.9 22.3 %copy-start.10 = (bf16[128]{0:T(256)(128)(2,1)S(1)}, bf16[128]{0:T(256)(128)(2,1)}, u32[]{:S(2)}) copy-start(bf16[128]{0:T(256)(128)(2,1)} %param.20) | copy-start | bytes 772
  179.9 26.6 %copy-start.4 = (bf16[128,256]{1,0:T(8,128)(2,1)S(1)}, bf16[128,256]{1,0:T(8,128)(2,1)}, u32[]{:S(2)}) copy-start(bf16[128,256]{1,0:T(8,128)(2,1)} %param.19) | copy-start | bytes 196612
  184.2 30.2 %collective-permute-start.2 = (bf16[2,256,1,512]{1,3,2,0:T(8,128)(2,1)}, bf16[2,256,1,512]{1,3,2,0:T(8,128)(2,1)S(1)}, u32[]{:S(2)}, u32[]{:S(2)}) collective-permute-start(bf16[2,256,1,512]{1,3,2,0:T(8,128)(2,1)} %get-tuple-element.9), channel_id=1, source_target_pairs={{0,1},{1,2},{2,3},{3,4},{4,5},{5,6},{6,7},{7,8},{8,9},{9,10},{10,1... | collective-permute-start | bytes 1572872 | tf_op jit(solution)/shard_map/ppermute | solution.py:21
  211.4 15.6 %collective-permute-start.3 = (bf16[2,256,1,512]{1,3,2,0:T(8,128)(2,1)}, bf16[2,256,1,512]{1,3,2,0:T(8,128)(2,1)S(1)}, u32[]{:S(2)}, u32[]{:S(2)}) collective-permute-start(bf16[2,256,1,512]{1,3,2,0:T(8,128)(2,1)} %get-tuple-element.10), channel_id=1, source_target_pairs={{1,0},{2,1},{3,2},{4,3},{5,4},{6,5},{7,6},{8,7},{9,8},{10,9},{11,1... | collective-permute-start | bytes 1572872 | tf_op jit(solution)/shard_map/ppermute | solution.py:23
  212.7 1.8 copy-start.3
  241.5 3.4 copy-start.1
Sparse Core Ops, SparseCore 0:
  9.9 47.6 all-gather.5
  141.0 33.2 all-gather.7
where the time goes:
time: 356 us; the launch traced here: 355 us
  blocking collectives  166 us (47%)
  waiting for transfers between devices  75.2 us (21%)
  matrix products  41.1 us (12%)
  local copies, waits for them, and re-layouts  27.1 us (8%)
  other arithmetic  21.5 us (6%)
  between operations  13.7 us (4%)
  starting transfers between devices  11 us (3%)
    psum x1, blocking collectives, per_device(): lax.psum(jnp.sum(deviation * deviation, 2), ('band', 'chan')) / pixel_count  40.9 us
    psum x1, blocking collectives, per_device(): out_mean = lax.psum(jnp.sum(conv_blocks, 2), ('band', 'chan')) / pixel_count  37 us
    all_to_all x1, waiting for transfers between devices, per_device(): lax.all_to_all(joined, 'chan', split_axis=2, concat_axis=1, tiled=True)  37 us
    psum x1, blocking collectives, per_device(): lat_mean = lax.psum(jnp.sum(lat_blocks, 2), 'band') / pixel_count  33.2 us
    dot_general x9, matrix products, conv_taps(): jnp.einsum('oc,ncrw->norw', taps_weight[row_tap, col_tap], window, prefer...  32.1 us
    psum x1, blocking collectives, per_device(): lat_var = lax.psum(jnp.sum(deviation * deviation, 2), 'band') / pixel_count  29.5 us
    all_gather x1, waiting for transfers between devices, per_device(): lax.all_gather(fine_features, 'chan', axis=1, tiled=True)  23.6 us
    ppermute x2, waiting for transfers between devices, extended_2(): lax.ppermute(head, axis, [((i + 1) % count, i) for i in range(ends)])  13.9 us
  transfers between devices with their start and end apart: 7, of which 4 were waited for; matrix products, arithmetic and copies ran while one was open for 7% of the time, Pallas kernels for 0%

commit v1 on v0

v1 whole, which is shorter than its diff:
```python
import functools

import jax
import jax.numpy as jnp
from jax import lax
from jax.experimental import pallas as pl
from jax.experimental.pallas import tpu as pltpu
from jax.sharding import PartitionSpec as P

D = 256
GROUPS = 32
EPS = 1e-05
MESH = pl.DeviceIdType.MESH
F32 = jnp.float32
BF16 = jnp.bfloat16


def wait_on(ref, sem):
    pltpu.make_async_copy(ref, ref, sem).wait()


def kernel(
    bands, chans, pixel_count,
    fine, coarse, early, late, queries,
    out,
    feats, level, ebuf, lbuf, lat, cols_up, stacked, conv, rows_out, stat1, stat2,
    f_send, f_recv, fh_send, fh_recv, c_send, c_recv, ch_send, ch_recv,
    w_send, w_recv, s_send, s_recv, o_sem,
):
    images, band_rows, in_ch, width = fine.shape
    rows = band_rows // chans
    c_rows = coarse.shape[1] // chans
    c_ch = coarse.shape[2]
    share = early.shape[0]
    gsize = D // GROUPS
    total = bands * chans
    b = lax.axis_index("band")
    c = lax.axis_index("chan")
    me = b * chans + c
    sends = []

    def send(src, dst, ssem, rsem, tb, tc, maybe_self):
        def remote():
            return pltpu.make_async_remote_copy(
                src_ref=src, dst_ref=dst, send_sem=ssem, recv_sem=rsem,
                device_id=(tb, tc), device_id_type=MESH,
            )

        if not maybe_self:
            remote().start()
            sends.append((remote, None))
            return
        is_self = jnp.logical_and(tb == b, tc == c)

        @pl.when(is_self)
        def _():
            pltpu.make_async_copy(src, dst, rsem).start()

        @pl.when(jnp.logical_not(is_self))
        def _():
            remote().start()

        sends.append((remote, is_self))

    def block(index, size):
        return pl.ds(pl.multiple_of(index * size, size), size)

    def gather(src, dst, ssem, rsem):
        pltpu.make_async_copy(src, dst.at[block(c, share)], rsem.at[0]).start()
        for s in range(1, chans):
            t = lax.rem(c + s, chans)
            send(src, dst.at[block(c, share)], ssem.at[s], rsem.at[s], b, t, False)

    def main_rows(src, dst, n, size, ch, ssem, rsem):
        for s in range(chans):
            t = lax.rem(c + s, chans)
            piece = src.at[n, pl.ds(t * size, size)]
            place = dst.at[n, pl.ds(1, size), block(c, ch)]
            if s == 0:
                pltpu.make_async_copy(piece, place, rsem.at[n, 0]).start()
            else:
                send(piece, place, ssem.at[n, s], rsem.at[n, s], b, t, False)

    def halo_rows(src, dst, n, size, ch, ssem, rsem):
        for s in range(chans):
            t = lax.rem(c + s, chans)
            k = (s + 1) % chans
            to = lax.rem(b * chans + t + 1, total)
            send(
                src.at[n, (t + 1) * size - 1], dst.at[n, 0, block(c, ch)],
                ssem.at[n, 0, s], rsem.at[n, 0, k], to // chans, lax.rem(to, chans), k == 0,
            )
            k = (s - 1) % chans
            to = lax.rem(b * chans + t - 1 + total, total)
            send(
                src.at[n, t * size], dst.at[n, size + 1, block(c, ch)],
                ssem.at[n, 1, s], rsem.at[n, 1, k], to // chans, lax.rem(to, chans), k == 0,
            )

    def wait_main(dst, n, size, ch, rsem):
        for s in range(chans):
            wait_on(dst.at[n, pl.ds(1, size), pl.ds(0, ch)], rsem.at[n, s])

    def wait_halo(dst, n, size, ch, rsem):
        for side in range(2):
            for s in range(chans):
                wait_on(dst.at[n, side * (size + 1), pl.ds(0, ch)], rsem.at[n, side, s])

    gather(early, ebuf, w_send.at[0], w_recv.at[0])
    for n in range(images):
        main_rows(fine, feats, n, rows, in_ch, f_send, f_recv)
    for n in range(images):
        halo_rows(fine, feats, n, rows, in_ch, fh_send, fh_recv)
        main_rows(coarse, level, n, c_rows, c_ch, c_send, c_recv)
        halo_rows(coarse, level, n, c_rows, c_ch, ch_send, ch_recv)
        if n == 0:
            gather(late, lbuf, w_send.at[1], w_recv.at[1])

    local_count = float(gsize * rows * width)
    lane = lax.broadcasted_iota(jnp.int32, (GROUPS, 128), 1)
    sub = lax.broadcasted_iota(jnp.int32, (GROUPS, 128), 0)
    eye = lane == sub
    tile_row = lax.broadcasted_iota(jnp.int32, (8, 128), 0)

    def group_sum(x):
        x = jnp.sum(x.reshape(GROUPS, gsize, x.shape[1]), axis=1)
        return jnp.sum(x, axis=1, keepdims=True)

    def to_channels(col):
        return jnp.broadcast_to(col[:, None, :], (GROUPS, gsize, 1)).reshape(D, 1)

    def to_row(col):
        return jnp.sum(jnp.where(eye, jnp.broadcast_to(col, (GROUPS, 128)), 0.0), axis=0, keepdims=True)

    def to_col(row):
        return jnp.sum(jnp.where(eye, jnp.broadcast_to(row, (GROUPS, 128)), 0.0), axis=1, keepdims=True)

    def local_stats(ref, n, first):
        s = group_sum(lax.fori_loop(
            0, rows, lambda r, acc: acc + ref[n, r + first], jnp.zeros((D, width), F32)))
        mean = to_channels(s / local_count)

        def step(r, acc):
            d = ref[n, r + first] - mean
            return acc + d * d

        m2 = group_sum(lax.fori_loop(0, rows, step, jnp.zeros((D, width), F32)))
        return to_row(s), to_row(m2)

    def exchange(stats, buf, which):
        tile = jnp.zeros((8, 128), F32)
        for n in range(images):
            for kind in range(2):
                tile = jnp.where(tile_row == kind * images + n, stats[n][kind], tile)
        buf[0] = tile

        def one(k, carry):
            to = lax.rem(me + k, total)
            pltpu.make_async_remote_copy(
                src_ref=buf.at[0], dst_ref=buf.at[k],
                send_sem=s_send.at[which], recv_sem=s_recv.at[which],
                device_id=(to // chans, lax.rem(to, chans)), device_id_type=MESH,
            ).start()
            return carry

        lax.fori_loop(1, total, one, 0)

    def combined(buf, which):
        wait_on(buf.at[pl.ds(1, total - 1)], s_recv.at[which])
        sums = buf[:, 0:images, :]
        m2s = buf[:, images:2 * images, :]
        mean = jnp.sum(sums, axis=0) / pixel_count
        off = sums / local_count - mean[None]
        var = (jnp.sum(m2s, axis=0) + local_count * jnp.sum(off * off, axis=0)) / pixel_count
        inv = lax.rsqrt(var + EPS)
        return [
            (to_channels(to_col(mean[n:n + 1])), to_channels(to_col(inv[n:n + 1])))
            for n in range(images)
        ]

    for s in range(chans):
        wait_on(ebuf.at[pl.ds(0, share)], w_recv.at[0, s])
    lat_w = ebuf[:, 0:in_ch * chans]
    params = ebuf[:, D:D + 128].astype(F32)
    lat_gain, lat_shift, out_gain, out_shift, bias = (params[:, k:k + 1] for k in range(5))

    stats = []
    for n in range(images):
        wait_main(feats, n, rows, in_ch, f_recv)

        def lateral(r, carry):
            lat[n, r + 1] = jnp.dot(lat_w, feats[n, r + 1], preferred_element_type=F32)
            return carry

        lax.fori_loop(0, rows, lateral, 0)
        stats.append(local_stats(lat, n, 1))
    exchange(stats, stat1, 0)

    src_col = lax.broadcasted_iota(jnp.int32, (width // 2, width), 0)
    dst_col = lax.broadcasted_iota(jnp.int32, (width // 2, width), 1)
    half = dst_col // 2
    near = jnp.where(src_col == half, 0.75, 0.0)
    other = jnp.clip(jnp.where(dst_col - 2 * half == 0, half - 1, half + 1), 0, width // 2 - 1)
    up = (near + jnp.where(src_col == other, 0.25, 0.0)).astype(BF16)
    lane_w = lax.broadcasted_iota(jnp.int32, (D, width), 1)

    norms = None
    for n in range(images):
        wait_halo(feats, n, rows, in_ch, fh_recv)
        for j in (0, rows + 1):
            lat[n, j] = jnp.dot(lat_w, feats[n, j], preferred_element_type=F32)
        wait_main(level, n, c_rows, c_ch, c_recv)
        wait_halo(level, n, c_rows, c_ch, ch_recv)

        def widen(k, carry):
            cols_up[k] = jnp.dot(level[n, k], up, preferred_element_type=F32)
            return carry

        lax.fori_loop(0, c_rows + 2, widen, 0)

        @pl.when(me == 0)
        def _():
            cols_up[0] = cols_up[1]

        @pl.when(me == total - 1)
        def _():
            cols_up[c_rows + 1] = cols_up[c_rows]

        if norms is None:
            norms = combined(stat1, 0)
        mean, inv = norms[n]
        scale = inv * lat_gain

        def join(j, carry):
            k = j // 2
            even = j - 2 * k == 0
            w0 = jnp.where(even, 0.75, 0.25)
            w1 = jnp.where(even, 0.25, 0.75)
            upsampled = w0 * cols_up[k] + w1 * cols_up[k + 1]
            joined = (lat[n, j] - mean) * scale + lat_shift + upsampled
            inside = jnp.logical_and(me * rows + j >= 1, me * rows + j <= total * rows)
            joined = jnp.where(inside, joined, 0.0)
            left = jnp.where(lane_w == 0, 0.0, pltpu.roll(joined, 1, 1))
            right = jnp.where(lane_w == width - 1, 0.0, pltpu.roll(joined, width - 1, 1))
            base = pl.multiple_of(j * 3 * D, D)
            stacked[pl.ds(base, D)] = left.astype(BF16)
            stacked[pl.ds(base + D, D)] = joined.astype(BF16)
            stacked[pl.ds(base + 2 * D, D)] = right.astype(BF16)
            return carry

        lax.fori_loop(0, rows + 2, join, 0)
        if n == 0:
            for s in range(chans):
                wait_on(lbuf.at[pl.ds(0, share)], w_recv.at[1, s])

        def convolve(r, carry):
            base = pl.multiple_of(r * 3 * D, D)
            conv[n, r] = jnp.dot(
                lbuf[:, 0:9 * D], stacked[pl.ds(base, 9 * D)], preferred_element_type=F32)
            return carry

        lax.fori_loop(0, rows, convolve, 0)

    exchange([local_stats(conv, n, 0) for n in range(images)], stat2, 1)
    norms = combined(stat2, 1)
    for n in range(images):
        mean, inv = norms[n]
        scale = inv * out_gain

        def finish(r, carry):
            act = jnp.maximum((conv[n, r] - mean) * scale + out_shift, 0.0).astype(BF16)
            mixed = jnp.dot(lbuf[:, 9 * D:10 * D], act, preferred_element_type=F32)
            features = (mixed + bias).astype(BF16)
            logits = jnp.dot(queries[...], features, preferred_element_type=F32)
            shifted = logits - jnp.max(logits, axis=0, keepdims=True)
            norm = jnp.log(jnp.sum(jnp.exp(shifted), axis=0, keepdims=True))
            rows_out[n, r] = shifted - norm
            pltpu.make_async_copy(rows_out.at[n, r], out.at[n, r], o_sem.at[n, r]).start()
            return carry

        lax.fori_loop(0, rows, finish, 0)

    for n in range(images):
        for r in range(rows):
            pltpu.make_async_copy(rows_out.at[n, r], out.at[n, r], o_sem.at[n, r]).wait()
    for which, buf in ((0, stat1), (1, stat2)):
        wait_on(buf.at[pl.ds(1, total - 1)], s_send.at[which])
    for remote, is_self in sends:
        if is_self is None:
            remote().wait_send()
        else:
            @pl.when(jnp.logical_not(is_self))
            def _():
                remote().wait_send()


def per_device(
    bands, chans,
    fine_features, coarse_level, lat_weight, lat_gain, lat_shift, out_weight, out_gain, out_shift,
    mask_weight, mask_bias, queries,
):
    images, in_ch, band_rows, width = fine_features.shape
    share = lat_weight.shape[0]
    c_ch, c_band = coarse_level.shape[1], coarse_level.shape[2]
    rows, c_rows = band_rows // chans, c_band // chans
    query_count = queries.shape[0]
    pixel_count = float(D // GROUPS * band_rows * bands * width)
    fine = jnp.transpose(fine_features, (0, 2, 1, 3))
    coarse = jnp.transpose(coarse_level, (0, 2, 1, 3))
    params = jnp.stack([lat_gain, lat_shift, out_gain, out_shift, mask_bias], axis=1)
    early = jnp.concatenate([
        jnp.pad(lat_weight, ((0, 0), (0, D - lat_weight.shape[1]))),
        jnp.pad(params, ((0, 0), (0, 128 - params.shape[1]))),
    ], axis=1)
    late = jnp.concatenate([
        jnp.transpose(out_weight, (2, 0, 1, 3)).reshape(share, 9 * D), mask_weight,
    ], axis=1)
    anywhere = pl.BlockSpec(memory_space=pl.ANY)
    vmem = pl.BlockSpec(memory_space=pltpu.VMEM)
    dma = pltpu.SemaphoreType.DMA
    result = pl.pallas_call(
        functools.partial(kernel, bands, chans, pixel_count),
        out_shape=jax.ShapeDtypeStruct((images, rows, query_count, width), F32),
        in_specs=[anywhere, anywhere, anywhere, anywhere, vmem],
        out_specs=anywhere,
        scratch_shapes=[
            pltpu.VMEM((images, rows + 2, chans * in_ch, width), BF16),
            pltpu.VMEM((images, c_rows + 2, chans * c_ch, width // 2), BF16),
            pltpu.VMEM((chans * share, early.shape[1]), BF16),
            pltpu.VMEM((chans * share, late.shape[1]), BF16),
            pltpu.VMEM((images, rows + 2, D, width), F32),
            pltpu.VMEM((c_rows + 2, D, width), F32),
            pltpu.VMEM(((rows + 2) * 3 * D, width), BF16),
            pltpu.VMEM((images, rows, D, width), F32),
            pltpu.VMEM((images, rows, query_count, width), F32),
            pltpu.VMEM((bands * chans, 8, 128), F32),
            pltpu.VMEM((bands * chans, 8, 128), F32),
            dma((images, chans)), dma((images, chans)),
            dma((images, 2, chans)), dma((images, 2, chans)),
            dma((images, chans)), dma((images, chans)),
            dma((images, 2, chans)), dma((images, 2, chans)),
            dma((2, chans)), dma((2, chans)),
            dma((2,)), dma((2,)),
            dma((images, rows)),
        ],
        compiler_params=pltpu.CompilerParams(
            has_side_effects=True, vmem_limit_bytes=60 * 1024 * 1024),
    )(fine, coarse, early, late, queries)
    return jnp.transpose(result, (0, 2, 1, 3))


def solution(mesh):
    return jax.shard_map(
        functools.partial(per_device, mesh.shape["band"], mesh.shape["chan"]),
        mesh=mesh,
        in_specs=(
            P(None, "chan", "band", None),
            P(None, "chan", "band", None),
            P("chan", None),
            P("chan"),
            P("chan"),
            P(None, None, "chan", None),
            P("chan"),
            P("chan"),
            P("chan", None),
            P("chan"),
            P(),
        ),
        out_specs=P(None, None, ("band", "chan"), None),
        check_vma=False,
    )
```

time: 356 us -> 108 us (0.30)
  blocking collectives: 166 us -> 0 us
  Pallas kernels: 0 us -> 94 us
  waiting for transfers between devices: 75.2 us -> 0 us
  matrix products: 41.1 us -> 0 us
  other arithmetic: 21.5 us -> 1.53 us
  local copies, waits for them, and re-layouts: 27.1 us -> 11.7 us
  between operations: 13.7 us -> 0.04 us
  starting transfers between devices: 11 us -> 0 us
    psum x4 -> x0, blocking collectives: 141 us -> none  [the longest x1 40.9 us: per_device(): lax.psum(jnp.sum(deviation * deviation, 2), ('band', 'chan')) / pixel_count]
    pallas_call x0 -> x1, Pallas kernels: none -> 94 us  [per_device(): pl.pallas_call(functools.partial(kernel, bands, chans, pixel_count), out_...]
    dot_general x11 -> x0, matrix products: 41.1 us -> none  [the longest x9 32.1 us: conv_taps(): jnp.einsum('oc,ncrw->norw', taps_weight[row_tap, col_tap], window, prefer...]
    all_to_all x1 -> x0, waiting for transfers between devices: 37 us -> none  [per_device(): lax.all_to_all(joined, 'chan', split_axis=2, concat_axis=1, tiled=True)]
    all_gather x4 -> x0, blocking collectives: 24.9 us -> none  [the longest x1 11.5 us: per_device(): lax.all_gather(out_gain, 'chan', axis=0, tiled=True)]
    all_gather x2 -> x0, waiting for transfers between devices: 23.6 us -> none  [the longest x1 23.6 us: per_device(): lax.all_gather(fine_features, 'chan', axis=1, tiled=True)]
    ppermute x4 -> x0, waiting for transfers between devices: 13.9 us -> none  [the longest x2 13.9 us: extended_2(): lax.ppermute(head, axis, [((i + 1) % count, i) for i in range(ends)])]
    another operation x2, local copies, waits for them, and re-layouts: 8.42 us -> 0.94 us  [per_device(): jnp.stack([lat_gain, lat_shift, out_gain, out_shift, mask_bias], axis=1)]
  transfers between devices with their start and end apart: 7 -> 0, of which waited for: 4 -> 0; matrix products, arithmetic and copies ran while one was open for 7% -> 0% of each run, Pallas kernels for 0% -> 0%
where the time goes in v1:
time: 108 us; the launch traced here: 107 us
  Pallas kernels  94 us (87%)
  local copies, waits for them, and re-layouts  11.7 us (11%)
  other arithmetic  1.53 us (1%)
    pallas_call x1, Pallas kernels, per_device(): pl.pallas_call(functools.partial(kernel, bands, chans, pixel_count), out_...  94 us
    transpose x1, local copies, waits for them, and re-layouts, per_device(): return jnp.transpose(result, (0, 2, 1, 3))  5.74 us
    unnamed x10, local copies, waits for them, and re-layouts  4.8 us

profile of v1, /device:TPU:0, one launch (start us, length us, event | category | flops | bytes accessed | tf_op | source)
XLA Modules:
  0.0 107.3 jit_solution(1704112737901400950)
XLA Ops:
  0.0 0.0 copy-start.1
  0.0 0.8 stack.23
  0.8 0.1 copy.36
  0.9 0.9 copy.35
  1.9 0.7 fusion.2.early
  2.5 0.0 copy-start.2
  2.5 1.9 %copy.43 = bf16[2,128,4,256]{3,1,2,0:T(8,128)(2,1)} copy(bf16[2,128,4,256]{3,2,1,0:T(4,128)(2,1)} %param.12) | data formatting | bytes 1048576 | tf_op args[1]
  4.5 0.0 copy-done.1
  4.5 0.0 copy-start
  4.5 0.3 copy.37
  4.8 0.3 copy.38
  5.0 0.0 copy-done.2
  5.0 0.9 pad_maximum_fusion.late
  5.9 0.0 copy-done
  5.9 1.6 %copy.42 = bf16[2,96,8,512]{3,1,2,0:T(8,128)(2,1)} copy(bf16[2,96,8,512]{3,2,1,0:T(8,128)(2,1)S(1)} %copy-done) | data formatting | bytes 3145728 | tf_op args[0]
  7.6 94.0 %shard_map.109 = f32[2,4,200,512]{3,2,1,0:T(8,128)} custom-call(bf16[2,8,96,512]{3,2,1,0:T(8,128)(2,1)} %bitcast.16, bf16[2,4,128,256]{3,2,1,0:T(8,128)(2,1)} %bitcast.18, bf16[128,384]{1,0:T(8,128)(2,1)} %fusion.2.early, bf16[128,2560]{1,0:T(8,128)(2,1)} %pad_maximum_fusion.late, bf16[200,256]{1,0:T(8,128)(2,1)} %queries.1), custom_call_target="tpu_custom_call" | custom-call | tf_op jit(solution)/shard_map/pallas_call | solution.py:321
  101.6 5.7 %copy.39 = f32[2,200,4,512]{3,2,1,0:T(4,128)} copy(f32[2,200,4,512]{3,1,2,0:T(8,128)} %bitcast.15) | data formatting | bytes 6553600 | tf_op jit(solution)/shard_map/transpose | solution.py:349
Async XLA Ops:
  0.0 4.5 %copy-start.1 = (bf16[3,3,128,256]{3,2,1,0:T(8,128)(2,1)S(1)}, bf16[3,3,128,256]{3,2,1,0:T(8,128)(2,1)}, u32[]{:S(2)}) copy-start(bf16[3,3,128,256]{3,2,1,0:T(8,128)(2,1)} %param.16) | copy-start | bytes 1769476
  2.5 2.5 %copy-start.2 = (bf16[128,256]{1,0:T(8,128)(2,1)S(1)}, bf16[128,256]{1,0:T(8,128)(2,1)}, u32[]{:S(2)}) copy-start(bf16[128,256]{1,0:T(8,128)(2,1)} %param.19) | copy-start | bytes 196612
  4.5 1.5 %copy-start = (bf16[2,96,8,512]{3,2,1,0:T(8,128)(2,1)S(1)}, bf16[2,96,8,512]{3,2,1,0:T(8,128)(2,1)}, u32[]{:S(2)}) copy-start(bf16[2,96,8,512]{3,2,1,0:T(8,128)(2,1)} %param.11) | copy-start | bytes 4718596

commit v2 on v1

--- a/solution.py
+++ b/solution.py
@@ -1,4 +1,5 @@
 import functools
+import math
 
 import jax
 import jax.numpy as jnp
@@ -21,17 +22,19 @@
 
 def kernel(
     bands, chans, pixel_count,
-    fine, coarse, early, late, queries,
+    fine, coarse, lat_in, par_in, conv_in, mask_in, queries,
     out,
-    feats, level, ebuf, lbuf, lat, cols_up, stacked, conv, rows_out, stat1, stat2,
+    feats, level, ebuf, pbuf, wbuf, mbuf, wide, lat, cols_up, stacked, conv, rows_out, stat1, stat2,
     f_send, f_recv, fh_send, fh_recv, c_send, c_recv, ch_send, ch_recv,
-    w_send, w_recv, s_send, s_recv, o_sem,
+    e_send, e_recv, w_send, w_recv, q_send, q_recv, s_send, s_recv, o_sem,
 ):
     images, band_rows, in_ch, width = fine.shape
     rows = band_rows // chans
     c_rows = coarse.shape[1] // chans
     c_ch = coarse.shape[2]
-    share = early.shape[0]
+    share = lat_in.shape[1]
+    quad = math.gcd(bands, 4)
+    quarter = share // quad
     gsize = D // GROUPS
     total = bands * chans
     b = lax.axis_index("band")
@@ -66,10 +69,39 @@
         return pl.ds(pl.multiple_of(index * size, size), size)
 
     def gather(src, dst, ssem, rsem):
-        pltpu.make_async_copy(src, dst.at[block(c, share)], rsem.at[0]).start()
+        pltpu.make_async_copy(src, dst.at[c], rsem.at[0]).start()
         for s in range(1, chans):
             t = lax.rem(c + s, chans)
-            send(src, dst.at[block(c, share)], ssem.at[s], rsem.at[s], b, t, False)
+            send(src, dst.at[c], ssem.at[s], rsem.at[s], b, t, False)
+
+    spot = lax.rem(b, quad)
+
+    def quarter_of(owner, part):
+        return pl.ds(pl.multiple_of(owner * share + part * quarter, quarter), quarter)
+
+    def weights_across(src, dst, ssem, rsem):
+        pltpu.make_async_copy(src, dst.at[:, block(c, share)], rsem.at[0]).start()
+        for s in range(1, chans):
+            t = lax.rem(c + s, chans)
+            send(
+                src.at[:, pl.ds(pl.multiple_of(spot * quarter, quarter), quarter)],
+                dst.at[:, quarter_of(c, spot)], ssem.at[s], rsem.at[s], b, t, False,
+            )
+
+    def weights_around(dst, rsem, ssem2, rsem2):
+        for s in range(1, chans):
+            wait_on(dst.at[:, pl.ds(0, quarter)], rsem.at[s])
+            owner = lax.rem(c - s + chans, chans)
+            piece = dst.at[:, quarter_of(owner, spot)]
+            for m in range(1, quad):
+                mate = b - spot + lax.rem(spot + m, quad)
+                send(piece, piece, ssem2.at[s, m], rsem2.at[s, m], mate, c, False)
+
+    def wait_weights(dst, rsem, rsem2):
+        wait_on(dst.at[:, pl.ds(0, share)], rsem.at[0])
+        for s in range(1, chans):
+            for m in range(1, quad):
+                wait_on(dst.at[:, pl.ds(0, quarter)], rsem2.at[s, m])
 
     def main_rows(src, dst, n, size, ch, ssem, rsem):
         for s in range(chans):
@@ -106,21 +138,23 @@
             for s in range(chans):
                 wait_on(dst.at[n, side * (size + 1), pl.ds(0, ch)], rsem.at[n, side, s])
 
-    gather(early, ebuf, w_send.at[0], w_recv.at[0])
+    gather(lat_in, ebuf, e_send.at[0], e_recv.at[0])
+    gather(par_in, pbuf, e_send.at[1], e_recv.at[1])
     for n in range(images):
         main_rows(fine, feats, n, rows, in_ch, f_send, f_recv)
-    for n in range(images):
-        halo_rows(fine, feats, n, rows, in_ch, fh_send, fh_recv)
-        main_rows(coarse, level, n, c_rows, c_ch, c_send, c_recv)
-        halo_rows(coarse, level, n, c_rows, c_ch, ch_send, ch_recv)
-        if n == 0:
-            gather(late, lbuf, w_send.at[1], w_recv.at[1])
+    weights_across(conv_in, wbuf, w_send.at[0], w_recv.at[0])
+    weights_across(mask_in, mbuf, w_send.at[1], w_recv.at[1])
+    halo_rows(fine, feats, 0, rows, in_ch, fh_send, fh_recv)
 
     local_count = float(gsize * rows * width)
     lane = lax.broadcasted_iota(jnp.int32, (GROUPS, 128), 1)
     sub = lax.broadcasted_iota(jnp.int32, (GROUPS, 128), 0)
-    eye = lane == sub
-    tile_row = lax.broadcasted_iota(jnp.int32, (8, 128), 0)
+
+    def fold(x):
+        acc = x[:, 0:128]
+        for k in range(1, width // 128):
+            acc = acc + x[:, k * 128:(k + 1) * 128]
+        return acc
 
     def group_sum(x):
         x = jnp.sum(x.reshape(GROUPS, gsize, x.shape[1]), axis=1)
@@ -129,30 +163,31 @@
     def to_channels(col):
         return jnp.broadcast_to(col[:, None, :], (GROUPS, gsize, 1)).reshape(D, 1)
 
-    def to_row(col):
-        return jnp.sum(jnp.where(eye, jnp.broadcast_to(col, (GROUPS, 128)), 0.0), axis=0, keepdims=True)
-
-    def to_col(row):
-        return jnp.sum(jnp.where(eye, jnp.broadcast_to(row, (GROUPS, 128)), 0.0), axis=1, keepdims=True)
-
-    def local_stats(ref, n, first):
-        s = group_sum(lax.fori_loop(
-            0, rows, lambda r, acc: acc + ref[n, r + first], jnp.zeros((D, width), F32)))
+    def at_lanes(col, slot):
+        return jnp.where(lane == sub + slot * GROUPS, jnp.broadcast_to(col, (GROUPS, 128)), 0.0)
+
+    def from_lanes(row, slot):
+        spread = jnp.where(lane == sub + slot * GROUPS, jnp.broadcast_to(row, (GROUPS, 128)), 0.0)
+        return jnp.sum(spread, axis=1, keepdims=True)
+
+    def produce(ref, n, first, compute):
+        def step(r, acc):
+            y = compute(r)
+            ref[n, r + first] = y
+            return acc + fold(y)
+
+        s = group_sum(lax.fori_loop(0, rows, step, jnp.zeros((D, 128), F32)))
         mean = to_channels(s / local_count)
 
-        def step(r, acc):
+        def spread(r, acc):
             d = ref[n, r + first] - mean
-            return acc + d * d
-
-        m2 = group_sum(lax.fori_loop(0, rows, step, jnp.zeros((D, width), F32)))
-        return to_row(s), to_row(m2)
+            return acc + fold(d * d)
+
+        m2 = group_sum(lax.fori_loop(0, rows, spread, jnp.zeros((D, 128), F32)))
+        return at_lanes(s, n) + at_lanes(m2, images + n)
 
     def exchange(stats, buf, which):
-        tile = jnp.zeros((8, 128), F32)
-        for n in range(images):
-            for kind in range(2):
-                tile = jnp.where(tile_row == kind * images + n, stats[n][kind], tile)
-        buf[0] = tile
+        buf[0] = jnp.sum(stats, axis=0, keepdims=True)
 
         def one(k, carry):
             to = lax.rem(me + k, total)
@@ -167,34 +202,55 @@
 
     def combined(buf, which):
         wait_on(buf.at[pl.ds(1, total - 1)], s_recv.at[which])
-        sums = buf[:, 0:images, :]
-        m2s = buf[:, images:2 * images, :]
-        mean = jnp.sum(sums, axis=0) / pixel_count
-        off = sums / local_count - mean[None]
-        var = (jnp.sum(m2s, axis=0) + local_count * jnp.sum(off * off, axis=0)) / pixel_count
+        parts = buf[...]
+        sums = jnp.sum(parts, axis=0)
+        mean = sums / pixel_count
+        off = parts / local_count - mean[None]
+        m2 = pltpu.roll(sums, 128 - images * GROUPS, 1)
+        var = (m2 + local_count * jnp.sum(off * off, axis=0)) / pixel_count
         inv = lax.rsqrt(var + EPS)
         return [
-            (to_channels(to_col(mean[n:n + 1])), to_channels(to_col(inv[n:n + 1])))
+            (to_channels(from_lanes(mean, n)), to_channels(from_lanes(inv, n)))
             for n in range(images)
         ]
 
-    for s in range(chans):
-        wait_on(ebuf.at[pl.ds(0, share)], w_recv.at[0, s])
-    lat_w = ebuf[:, 0:in_ch * chans]
-    params = ebuf[:, D:D + 128].astype(F32)
-    lat_gain, lat_shift, out_gain, out_shift, bias = (params[:, k:k + 1] for k in range(5))
-
-    stats = []
+    for k in range(2):
+        for s in range(chans):
+            wait_on((ebuf, pbuf)[k].at[0], e_recv.at[k, s])
+    square = (
+        lax.broadcasted_iota(jnp.int32, (share, share), 0)
+        == lax.broadcasted_iota(jnp.int32, (share, share), 1)
+    )
+
+    def column(k):
+        return jnp.concatenate([
+            jnp.sum(jnp.where(
+                square, jnp.broadcast_to(pbuf[s].astype(F32)[k:k + 1], (share, share)), 0.0,
+            ), axis=1, keepdims=True)
+            for s in range(chans)
+        ], axis=0)
+
+    lat_gain, lat_shift, out_gain, out_shift, bias = (column(k) for k in range(5))
+
+    def lateral(features):
+        return jnp.concatenate([
+            lax.dot_general(
+                ebuf[s], features, (((0,), (0,)), ((), ())), preferred_element_type=F32)
+            for s in range(chans)
+        ], axis=0)
+
+    stats = jnp.zeros((GROUPS, 128), F32)
     for n in range(images):
         wait_main(feats, n, rows, in_ch, f_recv)
-
-        def lateral(r, carry):
-            lat[n, r + 1] = jnp.dot(lat_w, feats[n, r + 1], preferred_element_type=F32)
-            return carry
-
-        lax.fori_loop(0, rows, lateral, 0)
-        stats.append(local_stats(lat, n, 1))
+        stats = stats + produce(lat, n, 1, lambda r, n=n: lateral(feats[n, r + 1]))
     exchange(stats, stat1, 0)
+    for n in range(images):
+        if n > 0:
+            halo_rows(fine, feats, n, rows, in_ch, fh_send, fh_recv)
+        main_rows(coarse, level, n, c_rows, c_ch, c_send, c_recv)
+        halo_rows(coarse, level, n, c_rows, c_ch, ch_send, ch_recv)
+    weights_around(wbuf, w_recv.at[0], q_send.at[0], q_recv.at[0])
+    weights_around(mbuf, w_recv.at[1], q_send.at[1], q_recv.at[1])
 
     src_col = lax.broadcasted_iota(jnp.int32, (width // 2, width), 0)
     dst_col = lax.broadcasted_iota(jnp.int32, (width // 2, width), 1)
@@ -204,11 +260,12 @@
     up = (near + jnp.where(src_col == other, 0.25, 0.0)).astype(BF16)
     lane_w = lax.broadcasted_iota(jnp.int32, (D, width), 1)
 
+    stats = jnp.zeros((GROUPS, 128), F32)
     norms = None
     for n in range(images):
         wait_halo(feats, n, rows, in_ch, fh_recv)
         for j in (0, rows + 1):
-            lat[n, j] = jnp.dot(lat_w, feats[n, j], preferred_element_type=F32)
+            lat[n, j] = lateral(feats[n, j])
         wait_main(level, n, c_rows, c_ch, c_recv)
         wait_halo(level, n, c_rows, c_ch, ch_recv)
 
@@ -250,18 +307,18 @@
 
         lax.fori_loop(0, rows + 2, join, 0)
         if n == 0:
-            for s in range(chans):
-                wait_on(lbuf.at[pl.ds(0, share)], w_recv.at[1, s])
-
-        def convolve(r, carry):
+            wait_weights(wbuf, w_recv.at[0], q_recv.at[0])
+            for k in range(9):
+                wide[:, k * D:(k + 1) * D] = wbuf[k]
+
+        def convolve(r):
             base = pl.multiple_of(r * 3 * D, D)
-            conv[n, r] = jnp.dot(
-                lbuf[:, 0:9 * D], stacked[pl.ds(base, 9 * D)], preferred_element_type=F32)
-            return carry
-
-        lax.fori_loop(0, rows, convolve, 0)
-
-    exchange([local_stats(conv, n, 0) for n in range(images)], stat2, 1)
+            return jnp.dot(wide[...], stacked[pl.ds(base, 9 * D)], preferred_element_type=F32)
+
+        stats = stats + produce(conv, n, 0, convolve)
+
+    exchange(stats, stat2, 1)
+    wait_weights(mbuf, w_recv.at[1], q_recv.at[1])
     norms = combined(stat2, 1)
     for n in range(images):
         mean, inv = norms[n]
@@ -269,7 +326,7 @@
 
         def finish(r, carry):
             act = jnp.maximum((conv[n, r] - mean) * scale + out_shift, 0.0).astype(BF16)
-            mixed = jnp.dot(lbuf[:, 9 * D:10 * D], act, preferred_element_type=F32)
+            mixed = jnp.dot(mbuf[0], act, preferred_element_type=F32)
             features = (mixed + bias).astype(BF16)
             logits = jnp.dot(queries[...], features, preferred_element_type=F32)
             shifted = logits - jnp.max(logits, axis=0, keepdims=True)
@@ -307,45 +364,46 @@
     pixel_count = float(D // GROUPS * band_rows * bands * width)
     fine = jnp.transpose(fine_features, (0, 2, 1, 3))
     coarse = jnp.transpose(coarse_level, (0, 2, 1, 3))
-    params = jnp.stack([lat_gain, lat_shift, out_gain, out_shift, mask_bias], axis=1)
-    early = jnp.concatenate([
-        jnp.pad(lat_weight, ((0, 0), (0, D - lat_weight.shape[1]))),
-        jnp.pad(params, ((0, 0), (0, 128 - params.shape[1]))),
-    ], axis=1)
-    late = jnp.concatenate([
-        jnp.transpose(out_weight, (2, 0, 1, 3)).reshape(share, 9 * D), mask_weight,
-    ], axis=1)
+    params = jnp.stack([lat_gain, lat_shift, out_gain, out_shift, mask_bias], axis=0)
+    params = jnp.pad(params, ((0, 16 - params.shape[0]), (0, 0)))
     anywhere = pl.BlockSpec(memory_space=pl.ANY)
     vmem = pl.BlockSpec(memory_space=pltpu.VMEM)
     dma = pltpu.SemaphoreType.DMA
     result = pl.pallas_call(
         functools.partial(kernel, bands, chans, pixel_count),
         out_shape=jax.ShapeDtypeStruct((images, rows, query_count, width), F32),
-        in_specs=[anywhere, anywhere, anywhere, anywhere, vmem],
+        in_specs=[anywhere] * 6 + [vmem],
         out_specs=anywhere,
         scratch_shapes=[
             pltpu.VMEM((images, rows + 2, chans * in_ch, width), BF16),
             pltpu.VMEM((images, c_rows + 2, chans * c_ch, width // 2), BF16),
-            pltpu.VMEM((chans * share, early.shape[1]), BF16),
-            pltpu.VMEM((chans * share, late.shape[1]), BF16),
+            pltpu.VMEM((chans, chans * in_ch, share), BF16),
+            pltpu.VMEM((chans, 16, share), BF16),
+            pltpu.VMEM((9, D, D), BF16),
+            pltpu.VMEM((1, D, D), BF16),
+            pltpu.VMEM((D, 9 * D), BF16),
             pltpu.VMEM((images, rows + 2, D, width), F32),
             pltpu.VMEM((c_rows + 2, D, width), F32),
             pltpu.VMEM(((rows + 2) * 3 * D, width), BF16),
             pltpu.VMEM((images, rows, D, width), F32),
             pltpu.VMEM((images, rows, query_count, width), F32),
-            pltpu.VMEM((bands * chans, 8, 128), F32),
-            pltpu.VMEM((bands * chans, 8, 128), F32),
+            pltpu.VMEM((bands * chans, 1, 128), F32),
+            pltpu.VMEM((bands * chans, 1, 128), F32),
             dma((images, chans)), dma((images, chans)),
             dma((images, 2, chans)), dma((images, 2, chans)),
             dma((images, chans)), dma((images, chans)),
             dma((images, 2, chans)), dma((images, 2, chans)),
-            dma((2, chans)), dma((2, chans)),
+            dma((2, chans)), dma((2, chans)), dma((2, chans)), dma((2, chans)),
+            dma((2, chans, 4)), dma((2, chans, 4)),
             dma((2,)), dma((2,)),
             dma((images, rows)),
         ],
         compiler_params=pltpu.CompilerParams(
             has_side_effects=True, vmem_limit_bytes=60 * 1024 * 1024),
-    )(fine, coarse, early, late, queries)
+    )(
+        fine, coarse, lat_weight.T, params, out_weight.reshape(9, share, D), mask_weight[None],
+        queries,
+    )
     return jnp.transpose(result, (0, 2, 1, 3))
 
 

time: 108 us -> 86.9 us (0.80)
  Pallas kernels: 94 us -> 74.6 us
  other arithmetic: 1.53 us -> 0 us
    pallas_call x1, Pallas kernels: 94 us -> 74.6 us  [per_device(): pl.pallas_call(functools.partial(kernel, bands, chans, pixel_count), out_...]
    concatenate x2 -> x0, other arithmetic: 1.53 us -> none  [the longest x1 0.88 us: per_device(): jnp.concatenate([jnp.transpose(out_weight, (2, 0, 1, 3)).reshape(share, 9...]
    unnamed x10 -> x2, local copies, waits for them, and re-layouts: 4.8 us -> 4.94 us
where the time goes in v2:
time: 86.9 us; the launch traced here: 86.7 us
  Pallas kernels  74.6 us (86%)
  local copies, waits for them, and re-layouts  12 us (14%)
    pallas_call x1, Pallas kernels, per_device(): pl.pallas_call(functools.partial(kernel, bands, chans, pixel_count), out_...  74.6 us
    transpose x1, local copies, waits for them, and re-layouts, per_device(): return jnp.transpose(result, (0, 2, 1, 3))  5.74 us
    unnamed x2, local copies, waits for them, and re-layouts  4.94 us

profile of v2, /device:TPU:0, one launch (start us, length us, event | category | flops | bytes accessed | tf_op | source)
XLA Modules:
  0.0 86.7 jit_solution(11345100425485186588)
XLA Ops:
  0.0 0.7 stack.23
  0.7 0.6 pad.4.par_in
  1.3 1.9 %copy.18 = bf16[2,128,4,256]{3,1,2,0:T(8,128)(2,1)} copy(bf16[2,128,4,256]{3,2,1,0:T(4,128)(2,1)} %param.12) | data formatting | bytes 1048576 | tf_op args[1]
  3.2 3.0 %copy.17 = bf16[2,96,8,512]{3,1,2,0:T(8,128)(2,1)} copy(bf16[2,96,8,512]{3,2,1,0:T(8,128)(2,1)} %param.11) | data formatting | bytes 3145728 | tf_op args[0]
  6.3 74.6 %shard_map.109 = f32[2,4,200,512]{3,2,1,0:T(8,128)} custom-call(bf16[2,8,96,512]{3,2,1,0:T(8,128)(2,1)} %bitcast.16, bf16[2,4,128,256]{3,2,1,0:T(8,128)(2,1)} %bitcast.17, bf16[192,128]{1,0:T(8,128)(2,1)} %bitcast.20, bf16[16,128]{1,0:T(8,128)(2,1)} %pad.4.par_in, bf16[9,128,256]{2,1,0:T(8,128)(2,1)} %bitcast.18, bf16[1,128,256]{2,1,0:T(8,128)(2,1)} %bitcast.19, ...), custom_call_target="tpu_custom_call" | custom-call | tf_op jit(solution)/shard_map/pallas_call | solution.py:372
  80.9 5.7 %copy.14 = f32[2,200,4,512]{3,2,1,0:T(4,128)} copy(f32[2,200,4,512]{3,1,2,0:T(8,128)} %bitcast.15) | data formatting | bytes 6553600 | tf_op jit(solution)/shard_map/transpose | solution.py:407

commit v3 on v2

--- a/solution.py
+++ b/solution.py
@@ -75,6 +75,7 @@
             send(src, dst.at[c], ssem.at[s], rsem.at[s], b, t, False)
 
     spot = lax.rem(b, quad)
+    near_count = quad * chans
 
     def quarter_of(owner, part):
         return pl.ds(pl.multiple_of(owner * share + part * quarter, quarter), quarter)
@@ -187,22 +188,35 @@
         return at_lanes(s, n) + at_lanes(m2, images + n)
 
     def exchange(stats, buf, which):
-        buf[0] = jnp.sum(stats, axis=0, keepdims=True)
-
-        def one(k, carry):
-            to = lax.rem(me + k, total)
+        buf[0, 0] = jnp.sum(stats, axis=0, keepdims=True)
+
+        def near_by(k, carry):
+            to = lax.rem(spot * chans + c + k, near_count)
+            pltpu.make_async_remote_copy(
+                src_ref=buf.at[0, 0], dst_ref=buf.at[0, k],
+                send_sem=s_send.at[which, 0], recv_sem=s_recv.at[which, 0],
+                device_id=(b - spot + to // chans, lax.rem(to, chans)), device_id_type=MESH,
+            ).start()
+            return carry
+
+        lax.fori_loop(1, near_count, near_by, 0)
+
+    def spread_out(buf, which):
+        wait_on(buf.at[0, pl.ds(1, near_count - 1)], s_recv.at[which, 0])
+
+        def far_off(k, carry):
             pltpu.make_async_remote_copy(
                 src_ref=buf.at[0], dst_ref=buf.at[k],
-                send_sem=s_send.at[which], recv_sem=s_recv.at[which],
-                device_id=(to // chans, lax.rem(to, chans)), device_id_type=MESH,
+                send_sem=s_send.at[which, 1], recv_sem=s_recv.at[which, 1],
+                device_id=(lax.rem(b + k * quad, bands), c), device_id_type=MESH,
             ).start()
             return carry
 
-        lax.fori_loop(1, total, one, 0)
+        lax.fori_loop(1, bands // quad, far_off, 0)
 
     def combined(buf, which):
-        wait_on(buf.at[pl.ds(1, total - 1)], s_recv.at[which])
-        parts = buf[...]
+        wait_on(buf.at[pl.ds(1, bands // quad - 1)], s_recv.at[which, 1])
+        parts = buf[...].reshape(total, 1, 128)
         sums = jnp.sum(parts, axis=0)
         mean = sums / pixel_count
         off = parts / local_count - mean[None]
@@ -251,6 +265,7 @@
         halo_rows(coarse, level, n, c_rows, c_ch, ch_send, ch_recv)
     weights_around(wbuf, w_recv.at[0], q_send.at[0], q_recv.at[0])
     weights_around(mbuf, w_recv.at[1], q_send.at[1], q_recv.at[1])
+    spread_out(stat1, 0)
 
     src_col = lax.broadcasted_iota(jnp.int32, (width // 2, width), 0)
     dst_col = lax.broadcasted_iota(jnp.int32, (width // 2, width), 1)
@@ -318,6 +333,7 @@
         stats = stats + produce(conv, n, 0, convolve)
 
     exchange(stats, stat2, 1)
+    spread_out(stat2, 1)
     wait_weights(mbuf, w_recv.at[1], q_recv.at[1])
     norms = combined(stat2, 1)
     for n in range(images):
@@ -341,7 +357,8 @@
         for r in range(rows):
             pltpu.make_async_copy(rows_out.at[n, r], out.at[n, r], o_sem.at[n, r]).wait()
     for which, buf in ((0, stat1), (1, stat2)):
-        wait_on(buf.at[pl.ds(1, total - 1)], s_send.at[which])
+        wait_on(buf.at[0, pl.ds(1, near_count - 1)], s_send.at[which, 0])
+        wait_on(buf.at[pl.ds(1, bands // quad - 1)], s_send.at[which, 1])
     for remote, is_self in sends:
         if is_self is None:
             remote().wait_send()
@@ -368,6 +385,7 @@
     params = jnp.pad(params, ((0, 16 - params.shape[0]), (0, 0)))
     anywhere = pl.BlockSpec(memory_space=pl.ANY)
     vmem = pl.BlockSpec(memory_space=pltpu.VMEM)
+    quad = math.gcd(bands, 4)
     dma = pltpu.SemaphoreType.DMA
     result = pl.pallas_call(
         functools.partial(kernel, bands, chans, pixel_count),
@@ -387,15 +405,15 @@
             pltpu.VMEM(((rows + 2) * 3 * D, width), BF16),
             pltpu.VMEM((images, rows, D, width), F32),
             pltpu.VMEM((images, rows, query_count, width), F32),
-            pltpu.VMEM((bands * chans, 1, 128), F32),
-            pltpu.VMEM((bands * chans, 1, 128), F32),
+            pltpu.VMEM((bands // quad, quad * chans, 1, 128), F32),
+            pltpu.VMEM((bands // quad, quad * chans, 1, 128), F32),
             dma((images, chans)), dma((images, chans)),
             dma((images, 2, chans)), dma((images, 2, chans)),
             dma((images, chans)), dma((images, chans)),
             dma((images, 2, chans)), dma((images, 2, chans)),
             dma((2, chans)), dma((2, chans)), dma((2, chans)), dma((2, chans)),
             dma((2, chans, 4)), dma((2, chans, 4)),
-            dma((2,)), dma((2,)),
+            dma((2, 2)), dma((2, 2)),
             dma((images, rows)),
         ],
         compiler_params=pltpu.CompilerParams(

time: 86.9 us -> 89 us (1.024)
  Pallas kernels: 74.6 us -> 76.7 us
    pallas_call x1, Pallas kernels: 74.6 us -> 76.7 us  [per_device(): pl.pallas_call(functools.partial(kernel, bands, chans, pixel_count), out_...]
where the time goes in v3:
time: 89 us; the launch traced here: 88.8 us
  Pallas kernels  76.7 us (86%)
  local copies, waits for them, and re-layouts  12 us (13%)
    pallas_call x1, Pallas kernels, per_device(): pl.pallas_call(functools.partial(kernel, bands, chans, pixel_count), out_...  76.7 us
    transpose x1, local copies, waits for them, and re-layouts, per_device(): return jnp.transpose(result, (0, 2, 1, 3))  5.74 us
    unnamed x2, local copies, waits for them, and re-layouts  4.94 us

profile of v3, /device:TPU:0, one launch (start us, length us, event | category | flops | bytes accessed | tf_op | source)
XLA Modules:
  0.0 88.8 jit_solution(6400082343675530871)
XLA Ops:
  0.0 0.7 stack.23
  0.7 0.6 pad.4.par_in
  1.3 1.9 %copy.18 = bf16[2,128,4,256]{3,1,2,0:T(8,128)(2,1)} copy(bf16[2,128,4,256]{3,2,1,0:T(4,128)(2,1)} %param.12) | data formatting | bytes 1048576 | tf_op args[1]
  3.2 3.0 %copy.17 = bf16[2,96,8,512]{3,1,2,0:T(8,128)(2,1)} copy(bf16[2,96,8,512]{3,2,1,0:T(8,128)(2,1)} %param.11) | data formatting | bytes 3145728 | tf_op args[0]
  6.3 76.7 %shard_map.109 = f32[2,4,200,512]{3,2,1,0:T(8,128)} custom-call(bf16[2,8,96,512]{3,2,1,0:T(8,128)(2,1)} %bitcast.16, bf16[2,4,128,256]{3,2,1,0:T(8,128)(2,1)} %bitcast.17, bf16[192,128]{1,0:T(8,128)(2,1)} %bitcast.20, bf16[16,128]{1,0:T(8,128)(2,1)} %pad.4.par_in, bf16[9,128,256]{2,1,0:T(8,128)(2,1)} %bitcast.18, bf16[1,128,256]{2,1,0:T(8,128)(2,1)} %bitcast.19, ...), custom_call_target="tpu_custom_call" | custom-call | tf_op jit(solution)/shard_map/pallas_call | solution.py:390
  83.0 5.7 %copy.14 = f32[2,200,4,512]{3,2,1,0:T(4,128)} copy(f32[2,200,4,512]{3,1,2,0:T(8,128)} %bitcast.15) | data formatting | bytes 6553600 | tf_op jit(solution)/shard_map/transpose | solution.py:425
